TPU v7x, 32 devices: a whole 2x2x4 slice. The times are simulated.
32 devices in a mesh: gx: 4 (over y, core), gy: 8 (over z, x).
Axes of the slice: x: 2, y: 2, z: 4, core: 2. Of those that a mesh axis runs over, the one named last changes fastest.
Arguments:
- emission: float32 [512, 8, 128], P(('gx', 'gy')), may hold values from 0.05 to 1
- reflectance: float32 [512, 8, 128], P(('gx', 'gy')), may hold values from 0.5 to 0.98
- form_factors: float32 [8192, 128, 128], P(('gx', 'gy')), as said below
- link_source: int32 [8192], P(('gx', 'gy')), may hold values from 0 to 511, as said below
- link_target: int32 [8192], P(('gx', 'gy')), may hold values from 0 to 511, as said below
- link_length: int32 [8192], P(('gx', 'gy')), may hold values from 32 to 128
- block_count: int32 [32], P(('gx', 'gy')), may hold values from 32 to 256, as said below
Outputs:
- solution: float32 [512, 8, 128], P(('gx', 'gy'))
- residual: float32 [512, 8, 128], P(('gx', 'gy'))
Inputs may be any that keep to these rules, and one draw needn't show every extreme that they name: `form_factors`: entries are nonnegative. `link_source`: block k's source is any cluster; among the blocks held by one device, all blocks whose sources lie on one same device name the same source cluster. `link_target`: block k's target is one of the clusters of the device holding it, clusters (k // 256) * 16 to (k // 256) * 16 + 15. `block_count`: some device has all 256 slots live.
All inputs are finite; a program needn't handle non-finite values.
Results may differ from a plain program's by a relative error of at most 0.0011.
Values sent between devices are 32-bit elements; how exact they have to be, the bound alone decides.
A program may use at most 64 MiB of HBM per device.

v0:
```python
import jax
import jax.numpy as jnp
from jax import lax
from jax.sharding import PartitionSpec as P

ITERS = 3


def local(emission, reflectance, form_factors, link_source, link_target, link_length, block_count):
    clusters = emission.shape[0]
    blocks = form_factors.shape[0]
    patch_count = form_factors.shape[2]
    devices = lax.axis_size(("gx", "gy"))
    group_size = min(16, blocks)
    live_count = block_count[0]
    block_ids = jnp.arange(blocks, dtype=jnp.int32)
    live_block = block_ids < live_count
    owner_dev = link_source // clusters
    local_slot = link_source % clusters
    peer_ids = jnp.arange(devices, dtype=jnp.int32)
    peer_match = (owner_dev[None, :] == peer_ids[:, None]) & live_block[None, :]
    wanted = jnp.max(jnp.where(peer_match, local_slot[None, :], 0), axis=1)
    want_from = lax.all_to_all(wanted, ("gx", "gy"), split_axis=0, concat_axis=0, tiled=True)
    column_ids = jnp.arange(patch_count, dtype=jnp.int32)
    column_mask = ((column_ids[None, :] < link_length[:, None]) & live_block[:, None]).astype(
        jnp.float32
    )
    cluster_ids = jnp.arange(clusters, dtype=jnp.int32)
    target_onehot = (cluster_ids[:, None] == (link_target % clusters)[None, :]).astype(jnp.float32)
    turn_count = (live_count + group_size - 1) // group_size

    def operate(radiance):
        outgoing = radiance[want_from]
        arrived = lax.all_to_all(outgoing, ("gx", "gy"), split_axis=0, concat_axis=0, tiled=True)
        sources = arrived[owner_dev] * column_mask[:, None, :]

        def turn(turn_index, total):
            first_block = turn_index * group_size
            factors = lax.dynamic_slice_in_dim(form_factors, first_block, group_size, 0)
            source_vals = lax.dynamic_slice_in_dim(sources, first_block, group_size, 0)
            onehot_part = lax.dynamic_slice_in_dim(target_onehot, first_block, group_size, 1)
            partial_sum = jnp.einsum(
                "kij,kbj->kbi", factors, source_vals, precision=lax.Precision.HIGHEST
            )
            return total + jnp.dot(
                onehot_part, partial_sum.reshape(group_size, -1), precision=lax.Precision.HIGHEST
            )

        empty_sum = jnp.zeros((clusters, radiance.shape[1] * radiance.shape[2]), jnp.float32)
        gathered = lax.fori_loop(0, turn_count, turn, empty_sum)
        return radiance - reflectance * gathered.reshape(radiance.shape)

    solution = jnp.zeros_like(emission)
    residual = emission
    direction = jnp.zeros_like(emission)
    applied = jnp.zeros_like(emission)
    rho_old = jnp.ones((), jnp.float32)
    alpha_coef = jnp.ones((), jnp.float32)
    omega_coef = jnp.ones((), jnp.float32)
    rho_now = lax.psum(jnp.sum(emission * residual), ("gx", "gy"))
    for iteration in range(ITERS):
        beta_coef = rho_now / rho_old * (alpha_coef / omega_coef)
        direction = residual + beta_coef * (direction - omega_coef * applied)
        applied = operate(direction)
        alpha_coef = rho_now / lax.psum(jnp.sum(emission * applied), ("gx", "gy"))
        middle = residual - alpha_coef * applied
        bounce = operate(middle)
        cross_sum, square_sum, shadow_middle, shadow_bounce = lax.psum(
            (
                jnp.sum(bounce * middle),
                jnp.sum(bounce * bounce),
                jnp.sum(emission * middle),
                jnp.sum(emission * bounce),
            ),
            ("gx", "gy"),
        )
        omega_coef = cross_sum / square_sum
        solution = solution + alpha_coef * direction + omega_coef * middle
        residual = middle - omega_coef * bounce
        rho_old = rho_now
        rho_now = shadow_middle - omega_coef * shadow_bounce
    return (solution, residual)


def solution(mesh):
    in_specs = (
        P(("gx", "gy"), None, None),
        P(("gx", "gy"), None, None),
        P(("gx", "gy"), None, None),
        P(("gx", "gy")),
        P(("gx", "gy")),
        P(("gx", "gy")),
        P(("gx", "gy")),
    )
    out_specs = (P(("gx", "gy"), None, None), P(("gx", "gy"), None, None))
    return jax.shard_map(local, mesh=mesh, in_specs=in_specs, out_specs=out_specs, check_vma=False)
```

profile of v0, /device:TPU:14, one launch (start us, length us, event | category | flops | bytes accessed | tf_op | source)
XLA Modules:
  0.0 708.0 jit_solution(13711820568220223381)
XLA Ops:
  2.9 1.5 multiply_reduce_fusion.13
  4.4 6.0 all-to-all-start
  10.3 40.6 %psum.98 = f32[]{:T(128)} all-reduce(f32[]{:T(128)} %multiply_reduce_fusion.13), channel_id=1, replica_groups=mesh['gx'=4,'gy'=8] {'gx','gy'}, use_global_device_ids=true, to_apply=%region_1.2 | all-reduce | flops 1 | bytes 8 | tf_op jit(solution)/shard_map/psum | solution.py:60
  53.9 1.2 gather_fusion
  55.1 4.8 all-to-all-start.1
  60.8 4.6 all-to-all-done.1
  66.6 16.3 %while.60 = (s32[]{:T(128)}, f32[16,1024]{1,0:T(8,128)S(1)}, s32[]{:T(128)}, f32[16,256]{1,0:T(8,128)S(1)}, f32[256,8,128]{2,1,0:T(8,128)S(1)}, /*index=5*/f32[2...) while((s32[]{:T(128)}, f32[16,1024]{1,0:T(8,128)S(1)}, s32[]{:T(128)}, ...), condition=%wide.region_4.5_spmd, body=%wide.region_3.4_spmd.sunk | while | flops 28327940 | bytes 1385623 | solution.py:50
  66.6 3.0 fusion.99
  69.9 3.0 fusion.99
  73.1 3.0 fusion.99
  76.4 3.0 fusion.99
  79.7 3.0 fusion.99
  82.9 1.5 multiply_reduce_fusion.12
  84.4 77.1 %psum.99 = f32[]{:T(128)} all-reduce(f32[]{:T(128)} %get-tuple-element.303), channel_id=1, replica_groups=mesh['gx'=4,'gy'=8] {'gx','gy'}, use_global_device_ids=true, to_apply=%region_6.7 | all-reduce | flops 1 | bytes 8 | tf_op jit(solution)/shard_map/psum | solution.py:65
  163.7 1.2 gather_fusion.2
  165.0 4.0 all-to-all-start.2
  169.0 5.5 all-to-all-done.2
  175.6 16.3 %while.61 = (s32[]{:T(128)}, f32[16,1024]{1,0:T(8,128)S(1)}, s32[]{:T(128)}, f32[16,256]{1,0:T(8,128)S(1)}, f32[256,8,128]{2,1,0:T(8,128)S(1)}, /*index=5*/f32[2...) while((s32[]{:T(128)}, f32[16,1024]{1,0:T(8,128)S(1)}, s32[]{:T(128)}, ...), condition=%wide.region_8.9_spmd, body=%wide.region_7.8_spmd.sunk | while | flops 28327940 | bytes 1385623 | solution.py:50
  175.6 3.0 fusion.104
  178.9 3.0 fusion.104
  182.2 3.0 fusion.104
  185.4 3.0 fusion.104
  188.7 3.0 fusion.104
  192.7 77.3 %all-reduce.2 = (f32[]{:T(128)}, f32[]{:T(128)}, f32[]{:T(128)}, f32[]{:T(128)}) all-reduce(f32[]{:T(128)} %get-tuple-element.215, f32[]{:T(128)} %get-tuple-element.214, f32[]{:T(128)} %get-tuple-element.213, f32[]{:T(128)} %get-tuple-element.212), channel_id=1, replica_groups=mesh['gx'=4,'gy'=8] {'gx','gy'}, use_global_device_ids=true, to_apply=%region_14.15 | all-reduce | flops 4 | bytes 32 | tf_op jit(solution)/shard_map/psum | solution.py:68
  275.8 1.2 gather_fusion.4
  277.0 4.0 all-to-all-start.3
  281.1 5.5 all-to-all-done.3
  287.7 16.3 %while.62 = (s32[]{:T(128)}, f32[16,1024]{1,0:T(8,128)S(1)}, s32[]{:T(128)}, f32[16,256]{1,0:T(8,128)S(1)}, f32[256,8,128]{2,1,0:T(8,128)S(1)}, /*index=5*/f32[2...) while((s32[]{:T(128)}, f32[16,1024]{1,0:T(8,128)S(1)}, s32[]{:T(128)}, ...), condition=%wide.region_18.19_spmd, body=%wide.region_17.18_spmd.sunk | while | flops 28327940 | bytes 1385623 | solution.py:50
  287.7 3.0 fusion.109
  291.0 3.0 fusion.109
  294.2 3.0 fusion.109
  297.5 3.0 fusion.109
  300.8 3.0 fusion.109
  304.7 77.1 %psum.104 = f32[]{:T(128)} all-reduce(f32[]{:T(128)} %get-tuple-element.300), channel_id=1, replica_groups=mesh['gx'=4,'gy'=8] {'gx','gy'}, use_global_device_ids=true, to_apply=%region_20.21 | all-reduce | flops 1 | bytes 8 | tf_op jit(solution)/shard_map/psum | solution.py:65
  382.5 1.2 gather_fusion.6
  383.7 4.0 all-to-all-start.4
  387.7 5.5 all-to-all-done.4
  394.3 16.5 %while.63 = (s32[]{:T(128)}, f32[16,1024]{1,0:T(8,128)S(1)}, s32[]{:T(128)}, f32[16,256]{1,0:T(8,128)S(1)}, f32[256,8,128]{2,1,0:T(8,128)S(1)}, /*index=5*/f32[2...) while((s32[]{:T(128)}, f32[16,1024]{1,0:T(8,128)S(1)}, s32[]{:T(128)}, ...), condition=%wide.region_22.23_spmd, body=%wide.region_21.22_spmd.sunk | while | flops 28327940 | bytes 1385623 | solution.py:50
  394.5 3.0 fusion.114
  397.8 3.0 fusion.114
  401.1 3.0 fusion.114
  404.3 3.0 fusion.114
  407.6 3.0 fusion.114
  411.6 77.3 %all-reduce.1 = (f32[]{:T(128)}, f32[]{:T(128)}, f32[]{:T(128)}, f32[]{:T(128)}) all-reduce(f32[]{:T(128)} %get-tuple-element.211, f32[]{:T(128)} %get-tuple-element.210, f32[]{:T(128)} %get-tuple-element.209, f32[]{:T(128)} %get-tuple-element.208), channel_id=1, replica_groups=mesh['gx'=4,'gy'=8] {'gx','gy'}, use_global_device_ids=true, to_apply=%region_28.29 | all-reduce | flops 4 | bytes 32 | tf_op jit(solution)/shard_map/psum | solution.py:68
  493.3 1.2 gather_fusion.8
  494.6 4.0 all-to-all-start.5
  498.6 5.5 all-to-all-done.5
  505.2 16.3 %while.64 = (s32[]{:T(128)}, f32[16,1024]{1,0:T(8,128)S(1)}, s32[]{:T(128)}, f32[16,256]{1,0:T(8,128)S(1)}, f32[256,8,128]{2,1,0:T(8,128)S(1)}, /*index=5*/f32[2...) while((s32[]{:T(128)}, f32[16,1024]{1,0:T(8,128)S(1)}, s32[]{:T(128)}, ...), condition=%wide.region_32.33_spmd, body=%wide.region_31.32_spmd.sunk | while | flops 28327940 | bytes 1385623 | solution.py:50
  505.2 3.0 fusion.119
  508.5 3.0 fusion.119
  511.8 3.0 fusion.119
  515.0 3.0 fusion.119
  518.3 3.0 fusion.119
  522.2 77.1 %psum.109 = f32[]{:T(128)} all-reduce(f32[]{:T(128)} %multiply_reduce_fusion.2), channel_id=1, replica_groups=mesh['gx'=4,'gy'=8] {'gx','gy'}, use_global_device_ids=true, to_apply=%region_34.35 | all-reduce | flops 1 | bytes 8 | tf_op jit(solution)/shard_map/psum | solution.py:65
  600.0 1.2 gather_fusion.10
  601.2 4.0 all-to-all-start.6
  605.3 5.5 all-to-all-done.6
  611.9 16.3 %while.65 = (s32[]{:T(128)}, f32[16,1024]{1,0:T(8,128)S(1)}, s32[]{:T(128)}, f32[16,256]{1,0:T(8,128)S(1)}, f32[256,8,128]{2,1,0:T(8,128)S(1)}, /*index=5*/f32[2...) while((s32[]{:T(128)}, f32[16,1024]{1,0:T(8,128)S(1)}, s32[]{:T(128)}, ...), condition=%wide.region_36.37_spmd, body=%wide.region_35.36_spmd.sunk | while | flops 28327940 | bytes 1385623 | solution.py:50
  611.9 3.0 fusion.124
  615.2 3.0 fusion.124
  618.4 3.0 fusion.124
  621.7 3.0 fusion.124
  625.0 3.0 fusion.124
  628.9 77.1 %all-reduce = (f32[]{:T(128)}, f32[]{:T(128)}) all-reduce(f32[]{:T(128)} %get-tuple-element.207, f32[]{:T(128)} %get-tuple-element.206), channel_id=1, replica_groups=mesh['gx'=4,'gy'=8] {'gx','gy'}, use_global_device_ids=true, to_apply=%region_38.39 | all-reduce | flops 2 | bytes 16 | tf_op jit(solution)/shard_map/psum | solution.py:68
  (82 shorter events, 24.8 us)
Async XLA Ops:
  0.6 191.3 %copy-start = (f32[16,8,128]{2,1,0:T(8,128)S(1)}, f32[16,8,128]{2,1,0:T(8,128)}, u32[]{:S(2)}) copy-start(f32[16,8,128]{2,1,0:T(8,128)} %param.19) | copy-start | bytes 196612
  0.6 191.3 %copy-start.1 = (f32[16,8,128]{2,1,0:T(8,128)S(1)}, f32[16,8,128]{2,1,0:T(8,128)}, u32[]{:S(2)}) copy-start(f32[16,8,128]{2,1,0:T(8,128)} %param.20) | copy-start | bytes 196612
  4.4 48.9 %all-to-all-start = ((s32[32,1,1]{2,1,0:T(1,128)}), s32[32,1,1]{2,1,0:T(1,128)S(1)}, u32[]{:S(2)}, u32[]{:S(2)}) async-start(s32[32,1,1]{2,1,0:T(1,128)} %copy.11), calls=%async_computation | async-start | bytes 32768 | tf_op jit(solution)/shard_map/all_to_all | solution.py:23
  55.1 10.3 %all-to-all-start.1 = ((f32[32,8,128]{2,1,0:T(8,128)}), f32[32,8,128]{2,1,0:T(8,128)S(1)}, u32[]{:S(2)}, u32[]{:S(2)}) async-start(f32[32,8,128]{2,1,0:T(8,128)} %gather_fusion), calls=%async_computation.1 | async-start | bytes 262144 | tf_op jit(solution)/shard_map/all_to_all | solution.py:34
  165.0 9.5 %all-to-all-start.2 = ((f32[32,8,128]{2,1,0:T(8,128)}), f32[32,8,128]{2,1,0:T(8,128)S(1)}, u32[]{:S(2)}, u32[]{:S(2)}) async-start(f32[32,8,128]{2,1,0:T(8,128)} %gather_fusion.2), calls=%async_computation.2 | async-start | bytes 262144 | tf_op jit(solution)/shard_map/all_to_all | solution.py:34
  277.0 9.5 %all-to-all-start.3 = ((f32[32,8,128]{2,1,0:T(8,128)}), f32[32,8,128]{2,1,0:T(8,128)S(1)}, u32[]{:S(2)}, u32[]{:S(2)}) async-start(f32[32,8,128]{2,1,0:T(8,128)} %gather_fusion.4), calls=%async_computation.3 | async-start | bytes 262144 | tf_op jit(solution)/shard_map/all_to_all | solution.py:34
  383.7 9.5 %all-to-all-start.4 = ((f32[32,8,128]{2,1,0:T(8,128)}), f32[32,8,128]{2,1,0:T(8,128)S(1)}, u32[]{:S(2)}, u32[]{:S(2)}) async-start(f32[32,8,128]{2,1,0:T(8,128)} %gather_fusion.6), calls=%async_computation.4 | async-start | bytes 262144 | tf_op jit(solution)/shard_map/all_to_all | solution.py:34
  494.6 9.5 %all-to-all-start.5 = ((f32[32,8,128]{2,1,0:T(8,128)}), f32[32,8,128]{2,1,0:T(8,128)S(1)}, u32[]{:S(2)}, u32[]{:S(2)}) async-start(f32[32,8,128]{2,1,0:T(8,128)} %gather_fusion.8), calls=%async_computation.5 | async-start | bytes 262144 | tf_op jit(solution)/shard_map/all_to_all | solution.py:34
  601.2 9.5 %all-to-all-start.6 = ((f32[32,8,128]{2,1,0:T(8,128)}), f32[32,8,128]{2,1,0:T(8,128)S(1)}, u32[]{:S(2)}, u32[]{:S(2)}) async-start(f32[32,8,128]{2,1,0:T(8,128)} %gather_fusion.10), calls=%async_computation.6 | async-start | bytes 262144 | tf_op jit(solution)/shard_map/all_to_all | solution.py:34
where the time goes:
time: 713 us; the launch traced here: 708 us
  blocking collectives  504 us (71%)
  matrix products  97 us (14%)
  waiting for transfers between devices  31.9 us (4%)
  starting transfers between devices  30.9 us (4%)
  between operations  16.7 us (2%)
  local copies, waits for them, and re-layouts  14.3 us (2%)
  other arithmetic  12.4 us (2%)
    psum x3, blocking collectives, local(): lax.psum((jnp.sum(bounce * middle), jnp.sum(bounce * bounce), jnp.sum(emi...  232 us
    psum x3, blocking collectives, local(): alpha_coef = rho_now / lax.psum(jnp.sum(emission * applied), ('gx', 'gy'))  231 us
    dot_general x30, matrix products, turn(): jnp.einsum('kij,kbj->kbi', factors, source_vals, precision=lax.Precision....  88.6 us
    psum x1, blocking collectives, local(): rho_now = lax.psum(jnp.sum(emission * residual), ('gx', 'gy'))  40.6 us
    all_to_all x6, waiting for transfers between devices, operate(): lax.all_to_all(outgoing, ('gx', 'gy'), split_axis=0, concat_axis=0, tiled...  31.9 us
    all_to_all x6, starting transfers between devices, operate(): lax.all_to_all(outgoing, ('gx', 'gy'), split_axis=0, concat_axis=0, tiled...  24.9 us
  transfers between devices with their start and end apart: 7, of which 6 were waited for; matrix products, arithmetic and copies ran while one was open for 0% of the time, Pallas kernels for 0%

commit v1 on v0

--- a/solution.py
+++ b/solution.py
@@ -66,13 +66,16 @@
         middle = residual - alpha_coef * applied
         bounce = operate(middle)
         cross_sum, square_sum, shadow_middle, shadow_bounce = lax.psum(
-            (
-                jnp.sum(bounce * middle),
-                jnp.sum(bounce * bounce),
-                jnp.sum(emission * middle),
-                jnp.sum(emission * bounce),
+            lax.psum(
+                (
+                    jnp.sum(bounce * middle),
+                    jnp.sum(bounce * bounce),
+                    jnp.sum(emission * middle),
+                    jnp.sum(emission * bounce),
+                ),
+                "gy",
             ),
-            ("gx", "gy"),
+            "gx",
         )
         omega_coef = cross_sum / square_sum
         solution = solution + alpha_coef * direction + omega_coef * middle

time: 713 us -> 671 us (0.941)
  the two profiles are of different devices: /device:TPU:14 before, /device:TPU:0 now
where the time goes in v1:
time: 671 us; the launch traced here: 666 us
  blocking collectives  481 us (72%)
  matrix products  58.2 us (9%)
  waiting for transfers between devices  46 us (7%)
  starting transfers between devices  36.3 us (5%)
  between operations  16.7 us (2%)
  local copies, waits for them, and re-layouts  14.3 us (2%)
  other arithmetic  12.5 us (2%)
    psum x3, blocking collectives, local(): alpha_coef = rho_now / lax.psum(jnp.sum(emission * applied), ('gx', 'gy'))  237 us
    psum x3, blocking collectives, local(): lax.psum((jnp.sum(bounce * middle), jnp.sum(bounce * bounce), jnp.sum(emi...  184 us
    dot_general x18, matrix products, turn(): jnp.einsum('kij,kbj->kbi', factors, source_vals, precision=lax.Precision....  53.1 us
    all_to_all x6, waiting for transfers between devices, operate(): lax.all_to_all(outgoing, ('gx', 'gy'), split_axis=0, concat_axis=0, tiled...  46 us
    psum x1, blocking collectives, local(): rho_now = lax.psum(jnp.sum(emission * residual), ('gx', 'gy'))  40.7 us
    all_to_all x6, starting transfers between devices, operate(): lax.all_to_all(outgoing, ('gx', 'gy'), split_axis=0, concat_axis=0, tiled...  29 us
    psum x3, blocking collectives, local(): lax.psum(lax.psum((jnp.sum(bounce * middle), jnp.sum(bounce * bounce), jn...  19.3 us
  transfers between devices with their start and end apart: 7, of which 6 were waited for; matrix products, arithmetic and copies ran while one was open for 0% of the time, Pallas kernels for 0%

profile of v1, /device:TPU:0, one launch (start us, length us, event | category | flops | bytes accessed | tf_op | source)
XLA Modules:
  0.0 665.7 jit_solution(17408464863754330313)
XLA Ops:
  2.9 1.5 multiply_reduce_fusion.13
  4.4 7.3 %all-to-all-start = ((s32[32,1,1]{2,1,0:T(1,128)}), s32[32,1,1]{2,1,0:T(1,128)S(1)}, u32[]{:S(2)}, u32[]{:S(2)}) async-start(s32[32,1,1]{2,1,0:T(1,128)} %copy.11), calls=%async_computation | async-start | bytes 32768 | tf_op jit(solution)/shard_map/all_to_all | solution.py:23
  11.7 40.7 %psum.168 = f32[]{:T(128)} all-reduce(f32[]{:T(128)} %multiply_reduce_fusion.13), channel_id=1, replica_groups=mesh['gx'=4,'gy'=8] {'gx','gy'}, use_global_device_ids=true, to_apply=%region_1.2 | all-reduce | flops 1 | bytes 8 | tf_op jit(solution)/shard_map/psum | solution.py:60
  53.1 0.8 broadcast_add_fusion
  55.4 1.2 gather_fusion
  56.6 4.7 all-to-all-start.1
  61.4 0.8 fusion.49
  62.2 7.0 %all-to-all-done.1 = f32[32,8,128]{2,1,0:T(8,128)S(1)} async-done(((f32[32,8,128]{2,1,0:T(8,128)}), f32[32,8,128]{2,1,0:T(8,128)S(1)}, u32[]{:S(2)}, u32[]{:S(2)}) %all-to-all-start.1) | async-done | bytes 131104 | tf_op jit(solution)/shard_map/all_to_all | solution.py:34
  69.1 1.0 gather_fusion.1
  70.3 9.8 %while.60 = (s32[]{:T(128)}, f32[16,1024]{1,0:T(8,128)S(1)}, s32[]{:T(128)}, f32[16,256]{1,0:T(8,128)S(1)}, f32[256,8,128]{2,1,0:T(8,128)S(1)}, /*index=5*/f32[2...) while((s32[]{:T(128)}, f32[16,1024]{1,0:T(8,128)S(1)}, s32[]{:T(128)}, ...), condition=%wide.region_4.5_spmd, body=%wide.region_3.4_spmd.sunk | while | flops 28327940 | bytes 1385623 | solution.py:50
  70.3 3.0 fusion.99
  73.6 3.0 fusion.99
  76.9 3.0 fusion.99
  80.1 1.5 multiply_reduce_fusion.12
  81.6 78.9 %psum.169 = f32[]{:T(128)} all-reduce(f32[]{:T(128)} %get-tuple-element.313), channel_id=1, replica_groups=mesh['gx'=4,'gy'=8] {'gx','gy'}, use_global_device_ids=true, to_apply=%region_6.7 | all-reduce | flops 1 | bytes 8 | tf_op jit(solution)/shard_map/psum | solution.py:65
  161.9 0.9 multiply_subtract_fusion.5
  162.8 1.2 gather_fusion.2
  164.0 6.4 all-to-all-start.2
  170.4 7.8 %all-to-all-done.2 = f32[32,8,128]{2,1,0:T(8,128)S(1)} async-done(((f32[32,8,128]{2,1,0:T(8,128)}), f32[32,8,128]{2,1,0:T(8,128)S(1)}, u32[]{:S(2)}, u32[]{:S(2)}) %all-to-all-start.2) | async-done | bytes 131104 | tf_op jit(solution)/shard_map/all_to_all | solution.py:34
  178.2 1.0 gather_fusion.3
  179.3 9.8 %while.61 = (s32[]{:T(128)}, f32[16,1024]{1,0:T(8,128)S(1)}, s32[]{:T(128)}, f32[16,256]{1,0:T(8,128)S(1)}, f32[256,8,128]{2,1,0:T(8,128)S(1)}, /*index=5*/f32[2...) while((s32[]{:T(128)}, f32[16,1024]{1,0:T(8,128)S(1)}, s32[]{:T(128)}, ...), condition=%wide.region_8.9_spmd, body=%wide.region_7.8_spmd.sunk | while | flops 28327940 | bytes 1385623 | solution.py:50
  179.4 3.0 fusion.104
  182.6 3.0 fusion.104
  185.9 3.0 fusion.104
  189.9 61.4 %all-reduce.2 = (f32[]{:T(128)}, f32[]{:T(128)}, f32[]{:T(128)}, f32[]{:T(128)}) all-reduce(f32[]{:T(128)} %get-tuple-element.215, f32[]{:T(128)} %get-tuple-element.214, f32[]{:T(128)} %get-tuple-element.213, f32[]{:T(128)} %get-tuple-element.212), channel_id=1, replica_groups=mesh['gx'=4,'gy'=8] {'gy'}, use_global_device_ids=true, to_apply=%region_16.17 | all-reduce | flops 4 | bytes 32 | tf_op jit(solution)/shard_map/psum | solution.py:69
  251.3 6.5 all-reduce.5
  263.6 1.2 gather_fusion.4
  264.8 2.6 all-to-all-start.3
  267.4 7.8 %all-to-all-done.3 = f32[32,8,128]{2,1,0:T(8,128)S(1)} async-done(((f32[32,8,128]{2,1,0:T(8,128)}), f32[32,8,128]{2,1,0:T(8,128)S(1)}, u32[]{:S(2)}, u32[]{:S(2)}) %all-to-all-start.3) | async-done | bytes 131104 | tf_op jit(solution)/shard_map/all_to_all | solution.py:34
  275.2 1.0 gather_fusion.5
  276.4 9.8 %while.62 = (s32[]{:T(128)}, f32[16,1024]{1,0:T(8,128)S(1)}, s32[]{:T(128)}, f32[16,256]{1,0:T(8,128)S(1)}, f32[256,8,128]{2,1,0:T(8,128)S(1)}, /*index=5*/f32[2...) while((s32[]{:T(128)}, f32[16,1024]{1,0:T(8,128)S(1)}, s32[]{:T(128)}, ...), condition=%wide.region_22.23_spmd, body=%wide.region_21.22_spmd.sunk | while | flops 28327940 | bytes 1385623 | solution.py:50
  276.4 3.0 fusion.109
  279.6 3.0 fusion.109
  282.9 3.0 fusion.109
  286.8 78.9 %psum.178 = f32[]{:T(128)} all-reduce(f32[]{:T(128)} %get-tuple-element.310), channel_id=1, replica_groups=mesh['gx'=4,'gy'=8] {'gx','gy'}, use_global_device_ids=true, to_apply=%region_24.25 | all-reduce | flops 1 | bytes 8 | tf_op jit(solution)/shard_map/psum | solution.py:65
  366.4 1.2 gather_fusion.6
  367.7 6.4 all-to-all-start.4
  374.0 7.8 %all-to-all-done.4 = f32[32,8,128]{2,1,0:T(8,128)S(1)} async-done(((f32[32,8,128]{2,1,0:T(8,128)}), f32[32,8,128]{2,1,0:T(8,128)S(1)}, u32[]{:S(2)}, u32[]{:S(2)}) %all-to-all-start.4) | async-done | bytes 131104 | tf_op jit(solution)/shard_map/all_to_all | solution.py:34
  381.9 1.0 gather_fusion.7
  383.0 10.0 %while.63 = (s32[]{:T(128)}, f32[16,1024]{1,0:T(8,128)S(1)}, s32[]{:T(128)}, f32[16,256]{1,0:T(8,128)S(1)}, f32[256,8,128]{2,1,0:T(8,128)S(1)}, /*index=5*/f32[2...) while((s32[]{:T(128)}, f32[16,1024]{1,0:T(8,128)S(1)}, s32[]{:T(128)}, ...), condition=%wide.region_26.27_spmd, body=%wide.region_25.26_spmd.sunk | while | flops 28327940 | bytes 1385623 | solution.py:50
  383.2 3.0 fusion.114
  386.5 3.0 fusion.114
  389.8 3.0 fusion.114
  393.8 61.4 %all-reduce.1 = (f32[]{:T(128)}, f32[]{:T(128)}, f32[]{:T(128)}, f32[]{:T(128)}) all-reduce(f32[]{:T(128)} %get-tuple-element.211, f32[]{:T(128)} %get-tuple-element.210, f32[]{:T(128)} %get-tuple-element.209, f32[]{:T(128)} %get-tuple-element.208), channel_id=1, replica_groups=mesh['gx'=4,'gy'=8] {'gy'}, use_global_device_ids=true, to_apply=%region_34.35 | all-reduce | flops 4 | bytes 32 | tf_op jit(solution)/shard_map/psum | solution.py:69
  455.2 6.5 all-reduce.4
  466.1 1.2 gather_fusion.8
  467.3 2.6 all-to-all-start.5
  469.9 7.8 %all-to-all-done.5 = f32[32,8,128]{2,1,0:T(8,128)S(1)} async-done(((f32[32,8,128]{2,1,0:T(8,128)}), f32[32,8,128]{2,1,0:T(8,128)S(1)}, u32[]{:S(2)}, u32[]{:S(2)}) %all-to-all-start.5) | async-done | bytes 131104 | tf_op jit(solution)/shard_map/all_to_all | solution.py:34
  477.7 1.0 gather_fusion.9
  478.8 9.8 %while.64 = (s32[]{:T(128)}, f32[16,1024]{1,0:T(8,128)S(1)}, s32[]{:T(128)}, f32[16,256]{1,0:T(8,128)S(1)}, f32[256,8,128]{2,1,0:T(8,128)S(1)}, /*index=5*/f32[2...) while((s32[]{:T(128)}, f32[16,1024]{1,0:T(8,128)S(1)}, s32[]{:T(128)}, ...), condition=%wide.region_40.41_spmd, body=%wide.region_39.40_spmd.sunk | while | flops 28327940 | bytes 1385623 | solution.py:50
  478.9 3.0 fusion.119
  482.1 3.0 fusion.119
  485.4 3.0 fusion.119
  489.3 78.9 %psum.187 = f32[]{:T(128)} all-reduce(f32[]{:T(128)} %multiply_reduce_fusion.2), channel_id=1, replica_groups=mesh['gx'=4,'gy'=8] {'gx','gy'}, use_global_device_ids=true, to_apply=%region_42.43 | all-reduce | flops 1 | bytes 8 | tf_op jit(solution)/shard_map/psum | solution.py:65
  568.9 1.2 gather_fusion.10
  570.1 6.4 all-to-all-start.6
  576.5 7.8 %all-to-all-done.6 = f32[32,8,128]{2,1,0:T(8,128)S(1)} async-done(((f32[32,8,128]{2,1,0:T(8,128)}), f32[32,8,128]{2,1,0:T(8,128)S(1)}, u32[]{:S(2)}, u32[]{:S(2)}) %all-to-all-start.6) | async-done | bytes 131104 | tf_op jit(solution)/shard_map/all_to_all | solution.py:34
  584.3 1.0 gather_fusion.11
  585.5 9.8 %while.65 = (s32[]{:T(128)}, f32[16,1024]{1,0:T(8,128)S(1)}, s32[]{:T(128)}, f32[16,256]{1,0:T(8,128)S(1)}, f32[256,8,128]{2,1,0:T(8,128)S(1)}, /*index=5*/f32[2...) while((s32[]{:T(128)}, f32[16,1024]{1,0:T(8,128)S(1)}, s32[]{:T(128)}, ...), condition=%wide.region_44.45_spmd, body=%wide.region_43.44_spmd.sunk | while | flops 28327940 | bytes 1385623 | solution.py:50
  585.5 3.0 fusion.124
  588.8 3.0 fusion.124
  592.0 3.0 fusion.124
  596.0 61.3 %all-reduce = (f32[]{:T(128)}, f32[]{:T(128)}) all-reduce(f32[]{:T(128)} %get-tuple-element.207, f32[]{:T(128)} %get-tuple-element.206), channel_id=1, replica_groups=mesh['gx'=4,'gy'=8] {'gy'}, use_global_device_ids=true, to_apply=%region_46.47 | all-reduce | flops 2 | bytes 16 | tf_op jit(solution)/shard_map/psum | solution.py:69
  657.3 6.4 all-reduce.3
  (61 shorter events, 12.8 us)
Async XLA Ops:
  0.6 188.5 %copy-start = (f32[16,8,128]{2,1,0:T(8,128)S(1)}, f32[16,8,128]{2,1,0:T(8,128)}, u32[]{:S(2)}) copy-start(f32[16,8,128]{2,1,0:T(8,128)} %param.19) | copy-start | bytes 196612
  0.6 188.5 %copy-start.1 = (f32[16,8,128]{2,1,0:T(8,128)S(1)}, f32[16,8,128]{2,1,0:T(8,128)}, u32[]{:S(2)}) copy-start(f32[16,8,128]{2,1,0:T(8,128)} %param.20) | copy-start | bytes 196612
  4.4 50.3 %all-to-all-start = ((s32[32,1,1]{2,1,0:T(1,128)}), s32[32,1,1]{2,1,0:T(1,128)S(1)}, u32[]{:S(2)}, u32[]{:S(2)}) async-start(s32[32,1,1]{2,1,0:T(1,128)} %copy.11), calls=%async_computation | async-start | bytes 32768 | tf_op jit(solution)/shard_map/all_to_all | solution.py:23
  56.6 12.6 %all-to-all-start.1 = ((f32[32,8,128]{2,1,0:T(8,128)}), f32[32,8,128]{2,1,0:T(8,128)S(1)}, u32[]{:S(2)}, u32[]{:S(2)}) async-start(f32[32,8,128]{2,1,0:T(8,128)} %gather_fusion), calls=%async_computation.1 | async-start | bytes 262144 | tf_op jit(solution)/shard_map/all_to_all | solution.py:34
  164.0 14.2 %all-to-all-start.2 = ((f32[32,8,128]{2,1,0:T(8,128)}), f32[32,8,128]{2,1,0:T(8,128)S(1)}, u32[]{:S(2)}, u32[]{:S(2)}) async-start(f32[32,8,128]{2,1,0:T(8,128)} %gather_fusion.2), calls=%async_computation.2 | async-start | bytes 262144 | tf_op jit(solution)/shard_map/all_to_all | solution.py:34
  264.8 10.4 %all-to-all-start.3 = ((f32[32,8,128]{2,1,0:T(8,128)}), f32[32,8,128]{2,1,0:T(8,128)S(1)}, u32[]{:S(2)}, u32[]{:S(2)}) async-start(f32[32,8,128]{2,1,0:T(8,128)} %gather_fusion.4), calls=%async_computation.3 | async-start | bytes 262144 | tf_op jit(solution)/shard_map/all_to_all | solution.py:34
  367.7 14.2 %all-to-all-start.4 = ((f32[32,8,128]{2,1,0:T(8,128)}), f32[32,8,128]{2,1,0:T(8,128)S(1)}, u32[]{:S(2)}, u32[]{:S(2)}) async-start(f32[32,8,128]{2,1,0:T(8,128)} %gather_fusion.6), calls=%async_computation.4 | async-start | bytes 262144 | tf_op jit(solution)/shard_map/all_to_all | solution.py:34
  467.3 10.4 %all-to-all-start.5 = ((f32[32,8,128]{2,1,0:T(8,128)}), f32[32,8,128]{2,1,0:T(8,128)S(1)}, u32[]{:S(2)}, u32[]{:S(2)}) async-start(f32[32,8,128]{2,1,0:T(8,128)} %gather_fusion.8), calls=%async_computation.5 | async-start | bytes 262144 | tf_op jit(solution)/shard_map/all_to_all | solution.py:34
  570.1 14.2 %all-to-all-start.6 = ((f32[32,8,128]{2,1,0:T(8,128)}), f32[32,8,128]{2,1,0:T(8,128)S(1)}, u32[]{:S(2)}, u32[]{:S(2)}) async-start(f32[32,8,128]{2,1,0:T(8,128)} %gather_fusion.10), calls=%async_computation.6 | async-start | bytes 262144 | tf_op jit(solution)/shard_map/all_to_all | solution.py:34
